TPU v7x, 32 devices: a whole 2x2x4 slice. The times are simulated.
32 devices in a mesh: sp: 4 (over x, core), tp: 8 (over z, y).
Axes of the slice: x: 2, y: 2, z: 4, core: 2. Of those that a mesh axis runs over, the one named last changes fastest.
Arguments:
- tokens: bfloat16 [8, 220, 4096], P(None, 'sp'), may hold values from -6 to 6
- modulation: float32 [6, 4096], replicated, may hold values from -2.5 to 2.5
- w_qkv: bfloat16 [4096, 3, 4096], P('sp', None, 'tp'), may hold values from -4 to 4
- w_out: bfloat16 [4096, 4096], P('tp', 'sp'), may hold values from -0.09375 to 0.09375
- w_up: bfloat16 [4096, 16384], P('sp', 'tp'), may hold values from -0.09375 to 0.09375
- w_down: bfloat16 [16384, 4096], P('tp', 'sp'), may hold values from -0.046875 to 0.046875
Outputs:
- block_out: bfloat16 [8, 220, 4096], P(None, 'sp', 'tp')
All inputs are finite; a program needn't handle non-finite values.
Results may differ from a plain program's by a relative error of at most 0.012.
Values may be sent and summed in bfloat16 or wider, within the bound.
No kernel may reach another device: no remote copies, remote signals or barrier semaphores. Data moves between devices by JAX's collectives and lax.ppermute only.
A program may use at most 128 MiB of HBM per device.

v0:
```python
import jax
import jax.numpy as jnp
from jax import lax
from jax.sharding import PartitionSpec as P

DH = 128
EPSILON = 1e-06


def normalize(tok_rows, shift_vec, scale_vec):
    values = tok_rows.astype(jnp.float32)
    center = jnp.mean(values, axis=-1, keepdims=True)
    spread = jnp.mean(jnp.square(values - center), axis=-1, keepdims=True)
    scaled = (values - center) * lax.rsqrt(spread + EPSILON)
    return (scaled * (1.0 + scale_vec) + shift_vec).astype(jnp.bfloat16)


def project_rows(operand, weight, einsum_form):
    return jnp.einsum(
        einsum_form,
        operand,
        lax.all_gather(weight, "sp", axis=0, tiled=True),
        preferred_element_type=jnp.float32,
    )


def project_cols(operand, weight, einsum_form, leading):
    portion = lax.all_gather(weight, "sp", axis=1, tiled=True)
    shaped = portion.reshape(leading + (portion.shape[1],))
    return jnp.einsum(einsum_form, operand, shaped, preferred_element_type=jnp.float32)


def attend_items(pieces):
    queries, key_rows, values = pieces
    factor = queries.shape[-1] ** (-0.5)

    def single(triple):
        query_one, key_one, value_one = triple
        scores = (
            lax.dot_general(
                query_one, key_one, (((1,), (1,)), ((), ())), preferred_element_type=jnp.float32
            )
            * factor
        )
        row_max = jnp.max(scores, axis=1, keepdims=True)
        raw_weights = jnp.exp(scores - row_max)
        att_weights = (raw_weights / jnp.sum(raw_weights, axis=1, keepdims=True)).astype(
            jnp.bfloat16
        )
        return jnp.dot(att_weights, value_one, preferred_element_type=jnp.float32).astype(
            jnp.bfloat16
        )

    result = lax.map(single, (queries[0], key_rows[0], values[0]))
    return result[None]


def attention_combine(base, partial_value, gate):
    summed = lax.psum(partial_value.astype(jnp.bfloat16), "tp").astype(jnp.float32)
    full = (base.astype(jnp.float32) + gate * summed).astype(jnp.bfloat16)
    return full


def mlp_combine(base, partial_value, gate):
    tp_count = lax.axis_size("tp")
    width = base.shape[2] // tp_count
    offset = lax.axis_index("tp") * width
    base_mine = lax.dynamic_slice_in_dim(base, offset, width, 2).astype(jnp.float32)
    gate_mine = lax.dynamic_slice_in_dim(gate, offset, width, 0)
    share = lax.psum_scatter(
        partial_value.astype(jnp.bfloat16), "tp", scatter_dimension=2, tiled=True
    ).astype(jnp.float32)
    return (base_mine + gate_mine * share).astype(jnp.bfloat16)


def shards(tokens, modulation, w_qkv, w_out, w_up, w_down):
    frames, patches, width = tokens.shape
    heads_local = w_qkv.shape[2] // DH
    sp_count = lax.axis_size("sp")
    items_dev = heads_local * frames // sp_count
    mod_a = normalize(tokens, modulation[0], modulation[1])
    weight_qkv = w_qkv.reshape(w_qkv.shape[0], 3, heads_local, DH)
    projected = project_rows(mod_a, weight_qkv, "fpd,dshe->shfpe").astype(jnp.bfloat16)
    projected = projected.reshape(3, sp_count, items_dev, patches, DH)
    attended = attend_items(
        (
            lax.all_to_all(projected[0], "sp", split_axis=0, concat_axis=2, tiled=True),
            lax.all_to_all(projected[1], "sp", split_axis=0, concat_axis=2, tiled=True),
            lax.all_to_all(projected[2], "sp", split_axis=0, concat_axis=2, tiled=True),
        )
    )
    returned = lax.all_to_all(attended, "sp", split_axis=2, concat_axis=0, tiled=True)
    returned = returned.reshape(heads_local, frames, patches, DH)
    partial_attn = project_cols(returned, w_out, "hfpd,hde->fpe", (heads_local, DH))
    middle = attention_combine(tokens, partial_attn, modulation[2])
    mod_b = normalize(middle, modulation[3], modulation[4])
    up_proj = project_rows(mod_b, w_up, "fpd,dc->fpc")
    hidden = jax.nn.gelu(up_proj, approximate=True).astype(jnp.bfloat16)
    partial_mlp = project_cols(hidden, w_down, "fpk,kc->fpc", (w_down.shape[0],))
    return mlp_combine(middle, partial_mlp, modulation[5])


def solution(mesh):
    placed = (
        P(None, "sp", None),
        P(),
        P("sp", None, "tp"),
        P("tp", "sp"),
        P("sp", "tp"),
        P("tp", "sp"),
    )
    return jax.shard_map(
        shards, mesh=mesh, in_specs=placed, out_specs=P(None, "sp", "tp"), check_vma=False
    )
```

profile of v0, /device:TPU:0, one launch (start us, length us, event | category | flops | bytes accessed | tf_op | source)
XLA Modules:
  0.0 655.9 jit_solution(7131236097919553995)
XLA Ops:
  6.5 3.2 copy.22
  9.7 2.8 copy.23
  13.4 5.8 convert_reduce_fusion
  19.2 3.9 fusion.23
  23.1 74.4 %all-gather.5.cloned.1.call-done = bf16[4096,3,4,128]{3,0,2,1:T(8,128)(2,1)} async-done(((bf16[1024,3,4,128]{3,0,2,1:T(8,128)(2,1)}), bf16[4096,3,4,128]{3,0,2,1:T(8,128)(2,1)}) %all-gather.5.cloned.1.call-update) | async-done | bytes 12582928 | tf_op jit(solution)/shard_map/all_gather | solution.py:22
  97.5 18.3 %fusion.69 = bf16[3,4,8,55,128]{4,3,1,0,2:T(8,128)(2,1)S(1)} fusion(bf16[4096,3,4,128]{3,0,2,1:T(8,128)(2,1)} %all-gather.5.cloned.1.call-done, f32[4096]{0:T(1024)S(1)} %bitcast.107, f32[4096]{0:T(1024)S(1)} %bitcast.108, f32[8,55]{1,0:T(8,128)S(1)} %add_rsqrt_fusion.1, f32[8,55]{1,0:T(8,128)S(1)} %broadcast_multiply_fusion.1, bf16[8,55,4096]{2,0,1:T(8,128)(2,1)} %param.8), kind=kOutput, calls=%fused_computation.64 | convolution fusion | flops 5547970560 | bytes 17575360 | tf_op jit(solution)/shard_map/fpd,dshe->shfpe/dot_general | solution.py:19
  116.9 3.5 all-to-all-start
  121.3 12.3 %all-to-all-done = bf16[4,8,55,128]{3,1,2,0:T(8,128)(2,1)S(1)} async-done(((bf16[4,8,55,128]{3,1,2,0:T(8,128)(2,1)}), bf16[4,8,55,128]{3,1,2,0:T(8,128)(2,1)S(1)}, u32[]{:S(2)}, u32[]{:S(2)}) %all-to-all-start) | async-done | bytes 450592 | tf_op jit(solution)/shard_map/all_to_all | solution.py:87
  133.6 3.5 all-to-all-start.1
  138.0 7.0 %all-to-all-done.1 = bf16[4,8,55,128]{3,1,2,0:T(8,128)(2,1)S(1)} async-done(((bf16[4,8,55,128]{3,1,2,0:T(8,128)(2,1)}), bf16[4,8,55,128]{3,1,2,0:T(8,128)(2,1)S(1)}, u32[]{:S(2)}, u32[]{:S(2)}) %all-to-all-start.1) | async-done | bytes 450592 | tf_op jit(solution)/shard_map/all_to_all | solution.py:88
  145.0 3.5 all-to-all-start.2
  148.7 7.8 %all-to-all-done.2 = bf16[4,8,55,128]{3,1,2,0:T(8,128)(2,1)S(1)} async-done(((bf16[4,8,55,128]{3,1,2,0:T(8,128)(2,1)}), bf16[4,8,55,128]{3,1,2,0:T(8,128)(2,1)S(1)}, u32[]{:S(2)}, u32[]{:S(2)}) %all-to-all-start.2) | async-done | bytes 450592 | tf_op jit(solution)/shard_map/all_to_all | solution.py:89
  156.6 4.6 while.10
  162.1 3.5 all-to-all-start.3
  165.6 7.9 %all-to-all-done.3 = bf16[1,8,220,128]{3,1,0,2:T(8,128)(2,1)S(1)} async-done(((bf16[1,8,220,128]{3,1,0,2:T(8,128)(2,1)}), bf16[1,8,220,128]{3,1,0,2:T(8,128)(2,1)S(1)}, u32[]{:S(2)}, u32[]{:S(2)}) %all-to-all-start.3) | async-done | bytes 450592 | tf_op jit(solution)/shard_map/all_to_all | solution.py:92
  173.6 5.7 bitcast_convert_fusion
  180.8 141.6 %all-reduce.2.cloned.1.call-done = bf16[8,55,4096]{2,1,0:T(8,128)(2,1)} async-done(((bf16[8,55,4096]{2,1,0:T(8,128)(2,1)}), bf16[8,55,4096]{2,1,0:T(8,128)(2,1)}) %all-reduce.2.cloned.1.call-update) | async-done | bytes 3604496 | tf_op jit(solution)/shard_map/psum | solution.py:59
  322.4 8.3 %convert_reduce_fusion.1 = (f32[8,55]{1,0:T(8,128)S(1)}, bf16[8,55,4096]{2,1,0:T(8,128)(2,1)S(1)}) fusion(bf16[8,55,4096]{2,1,0:T(8,128)(2,1)} %all-reduce.2.cloned.1.call-done, f32[4096]{0:T(1024)S(1)} %bitcast.104, bf16[8,55,4096]{2,0,1:T(8,128)(2,1)} %param.8), kind=kLoop, calls=%fused_computation.27 | loop fusion | flops 12615240 | bytes 10831584 | tf_op jit(solution)/shard_map/reduce_sum | solution.py:12
  330.7 2.0 copy-done.1
  333.8 94.7 %all-gather.11.cloned.1.call-done = bf16[2048,4096]{1,0:T(8,128)(2,1)} async-done(((bf16[2048,1024]{1,0:T(8,128)(2,1)}), bf16[2048,4096]{1,0:T(8,128)(2,1)}) %all-gather.11.cloned.1.call-update) | async-done | bytes 16777232 | tf_op jit(solution)/shard_map/all_gather | solution.py:28
  428.5 107.3 %all-gather.9.cloned.1.call-done = bf16[4096,2048]{1,0:T(8,128)(2,1)} async-done(((bf16[1024,2048]{1,0:T(8,128)(2,1)}), bf16[4096,2048]{1,0:T(8,128)(2,1)}) %all-gather.9.cloned.1.call-update) | async-done | bytes 16777232 | tf_op jit(solution)/shard_map/all_gather | solution.py:22
  535.9 29.4 %fusion.32 = bf16[8,55,4096]{2,1,0:T(8,128)(2,1)} fusion(bf16[2048,4096]{1,0:T(8,128)(2,1)} %all-gather.11.cloned.1.call-done, bf16[4096,2048]{1,0:T(8,128)(2,1)} %all-gather.9.cloned.1.call-done, bf16[8,55,4096]{2,1,0:T(8,128)(2,1)} %copy-done.1, f32[4096]{0:T(1024)S(1)} %bitcast.105, f32[4096]{0:T(1024)S(1)} %bitcast.106, f32[8,55]{1,0:T(8,128)S(1)} %add_rsqrt_fusion, ...), kind=kOutput, calls=%fused_computation.42 | convolution fusion | flops 14784675840 | bytes 40799680 | tf_op jit(solution)/shard_map/fpk,kc->fpc/dot_general | solution.py:30
  565.4 81.5 %reduce-scatter.2.cloned.1.call-done = bf16[8,55,512]{2,1,0:T(8,128)(2,1)} async-done(((bf16[8,55,4096]{2,1,0:T(8,128)(2,1)}), bf16[8,55,512]{2,1,0:T(8,128)(2,1)}) %reduce-scatter.2.cloned.1.call-update) | async-done | bytes 450576 | tf_op jit(solution)/shard_map/reduce_scatter | solution.py:70
  646.9 1.3 add_convert_fusion
  (59 shorter events, 12.9 us)
Async XLA Ops:
  6.5 91.0 %all-gather.5.cloned.1.call-start = ((), (), s32[]{:S(2)}) async-start(), calls=%async_computation.5 | async-start | bytes 15728640 | tf_op jit(solution)/shard_map/all_gather | solution.py:22
  9.7 3.6 copy-start.2
  12.6 153.1 %all-gather.7.cloned.1.call-start = ((), (), s32[]{:S(2)}) async-start(), calls=%async_computation.6 | async-start | bytes 5242880 | tf_op jit(solution)/shard_map/all_gather | solution.py:28
  13.3 5.9 copy-start
  116.9 16.7 %all-to-all-start = ((bf16[4,8,55,128]{3,1,2,0:T(8,128)(2,1)}), bf16[4,8,55,128]{3,1,2,0:T(8,128)(2,1)S(1)}, u32[]{:S(2)}, u32[]{:S(2)}) async-start(bf16[4,8,55,128]{3,1,2,0:T(8,128)(2,1)} %copy.24), calls=%async_computation | async-start | bytes 901120 | tf_op jit(solution)/shard_map/all_to_all | solution.py:87
  133.6 11.5 %all-to-all-start.1 = ((bf16[4,8,55,128]{3,1,2,0:T(8,128)(2,1)}), bf16[4,8,55,128]{3,1,2,0:T(8,128)(2,1)S(1)}, u32[]{:S(2)}, u32[]{:S(2)}) async-start(bf16[4,8,55,128]{3,1,2,0:T(8,128)(2,1)} %copy.25), calls=%async_computation.1 | async-start | bytes 901120 | tf_op jit(solution)/shard_map/all_to_all | solution.py:88
  145.0 11.5 %all-to-all-start.2 = ((bf16[4,8,55,128]{3,1,2,0:T(8,128)(2,1)}), bf16[4,8,55,128]{3,1,2,0:T(8,128)(2,1)S(1)}, u32[]{:S(2)}, u32[]{:S(2)}) async-start(bf16[4,8,55,128]{3,1,2,0:T(8,128)(2,1)} %copy.26), calls=%async_computation.2 | async-start | bytes 901120 | tf_op jit(solution)/shard_map/all_to_all | solution.py:89
  162.1 11.5 %all-to-all-start.3 = ((bf16[1,8,220,128]{3,1,0,2:T(8,128)(2,1)}), bf16[1,8,220,128]{3,1,0,2:T(8,128)(2,1)S(1)}, u32[]{:S(2)}, u32[]{:S(2)}) async-start(bf16[1,8,220,128]{3,1,0,2:T(8,128)(2,1)} %bitcast.90), calls=%async_computation.3 | async-start | bytes 901120 | tf_op jit(solution)/shard_map/all_to_all | solution.py:92
  165.6 156.8 %all-reduce.2.cloned.1.call-start = ((), (), s32[]{:S(2)}) async-start(), calls=%async_computation.7 | async-start | bytes 7340032 | tf_op jit(solution)/shard_map/psum | solution.py:59
  179.3 249.2 %all-gather.11.cloned.1.call-start = ((), (), s32[]{:S(2)}) async-start(), calls=%async_computation.9 | async-start | bytes 20971520 | tf_op jit(solution)/shard_map/all_gather | solution.py:28
  179.9 356.0 %all-gather.9.cloned.1.call-start = ((), (), s32[]{:S(2)}) async-start(), calls=%async_computation.8 | async-start | bytes 20971520 | tf_op jit(solution)/shard_map/all_gather | solution.py:22
  180.5 466.4 %reduce-scatter.2.cloned.1.call-start = ((), (), s32[]{:S(2)}) async-start(), calls=%async_computation.10 | async-start | bytes 4128768 | tf_op jit(solution)/shard_map/reduce_scatter | solution.py:70
  330.7 2.0 copy-start.1
Sparse Core Ops, SparseCore 0:
  12.7 84.7 all-gather.4
  99.1 39.4 all-gather.6
  179.4 142.8 all-reduce.1
  323.8 104.7 all-gather.10
  429.9 105.8 all-gather.8
  565.5 81.3 reduce-scatter.1
where the time goes:
time: 656 us
  waiting for transfers between devices  536 us (82%)
  matrix products  57.3 us (9%)
  other arithmetic  21.1 us (3%)
  starting transfers between devices  14.3 us (2%)
  between operations  13.6 us (2%)
  local copies, waits for them, and re-layouts  13 us (2%)
    all_gather x2, waiting for transfers between devices, project_rows(): lax.all_gather(weight, 'sp', axis=0, tiled=True)  182 us
    psum x1, waiting for transfers between devices, attention_combine(): lax.psum(partial_value.astype(jnp.bfloat16), 'tp').astype(jnp.float32)  142 us
    all_gather x2, waiting for transfers between devices, project_cols(): portion = lax.all_gather(weight, 'sp', axis=1, tiled=True)  94.7 us
    reduce_scatter x1, waiting for transfers between devices, mlp_combine(): lax.psum_scatter(partial_value.astype(jnp.bfloat16), 'tp', scatter_dimens...  81.5 us
    dot_general x2, matrix products, project_cols(): jnp.einsum(einsum_form, operand, shaped, preferred_element_type=jnp.float32)  35.2 us
    dot_general x1, matrix products, project_rows(): jnp.einsum(einsum_form, operand, lax.all_gather(weight, 'sp', axis=0, til...  18.3 us
    reduce_sum x2, other arithmetic, normalize(): center = jnp.mean(values, axis=-1, keepdims=True)  14.1 us
  transfers between devices with their start and end apart: 10, of which 9 were waited for; matrix products, arithmetic and copies ran while one was open for 7% of the time, Pallas kernels for 0%

commit v1 on v0

--- a/solution.py
+++ b/solution.py
@@ -1,10 +1,20 @@
+import functools
 import jax
 import jax.numpy as jnp
 from jax import lax
 from jax.sharding import PartitionSpec as P
+from jax.lax import all_gather
 
 DH = 128
 EPSILON = 1e-06
+
+
+def _tell_spots(piece_in, dev_axis):
+    prior = jnp.sum(all_gather(piece_in, axis_name=dev_axis), axis=0)
+    return prior
+
+
+sides_do = functools.partial(_tell_spots, dev_axis="tp")
 
 
 def normalize(tok_rows, shift_vec, scale_vec):
@@ -56,7 +66,7 @@
 
 
 def attention_combine(base, partial_value, gate):
-    summed = lax.psum(partial_value.astype(jnp.bfloat16), "tp").astype(jnp.float32)
+    summed = sides_do(partial_value.astype(jnp.bfloat16)).astype(jnp.float32)
     full = (base.astype(jnp.float32) + gate * summed).astype(jnp.bfloat16)
     return full
 

time: 656 us -> 1070 us (1.63)
  waiting for transfers between devices: 536 us -> 923 us
  other arithmetic: 21.1 us -> 42 us
    all_gather x0 -> x1, waiting for transfers between devices: none -> 548 us  [_tell_spots(): prior = jnp.sum(all_gather(piece_in, axis_name=dev_axis), axis=0)]
    psum x1 -> x0, waiting for transfers between devices: 142 us -> none  [attention_combine(): lax.psum(partial_value.astype(jnp.bfloat16), 'tp').astype(jnp.float32)]
    all_gather x2, waiting for transfers between devices: 182 us -> 149 us  [project_rows(): lax.all_gather(weight, 'sp', axis=0, tiled=True)]
    reduce_sum x0 -> x1, other arithmetic: none -> 14.2 us  [_tell_spots(): prior = jnp.sum(all_gather(piece_in, axis_name=dev_axis), axis=0)]
    all_gather x2, waiting for transfers between devices: 94.7 us -> 107 us  [project_cols(): portion = lax.all_gather(weight, 'sp', axis=1, tiled=True)]
  transfers between devices with their start and end apart: 10 -> 10, of which waited for: 9 -> 9; matrix products, arithmetic and copies ran while one was open for 7% -> 6% of each run, Pallas kernels for 0% -> 0%
where the time goes in v1:
time: 1070 us
  waiting for transfers between devices  923 us (86%)
  matrix products  56.9 us (5%)
  other arithmetic  42 us (4%)
  local copies, waits for them, and re-layouts  16.6 us (2%)
  starting transfers between devices  14.2 us (1%)
  between operations  13.9 us (1%)
    all_gather x1, waiting for transfers between devices, _tell_spots(): prior = jnp.sum(all_gather(piece_in, axis_name=dev_axis), axis=0)  548 us
    all_gather x2, waiting for transfers between devices, project_rows(): lax.all_gather(weight, 'sp', axis=0, tiled=True)  149 us
    all_gather x2, waiting for transfers between devices, project_cols(): portion = lax.all_gather(weight, 'sp', axis=1, tiled=True)  107 us
    reduce_scatter x1, waiting for transfers between devices, mlp_combine(): lax.psum_scatter(partial_value.astype(jnp.bfloat16), 'tp', scatter_dimens...  81.5 us
    dot_general x2, matrix products, project_cols(): jnp.einsum(einsum_form, operand, shaped, preferred_element_type=jnp.float32)  34.3 us
  transfers between devices with their start and end apart: 10, of which 9 were waited for; matrix products, arithmetic and copies ran while one was open for 6% of the time, Pallas kernels for 0%

profile of v1, /device:TPU:0, one launch (start us, length us, event | category | flops | bytes accessed | tf_op | source)
XLA Modules:
  0.0 1067.0 jit_solution(6587318291457277410)
XLA Ops:
  6.5 3.2 copy.35
  9.7 2.8 copy.36
  13.4 5.8 convert_reduce_fusion
  19.2 3.9 fusion.23
  23.1 74.4 %all-gather.7.cloned.1.call-done = bf16[4096,3,4,128]{3,0,2,1:T(8,128)(2,1)} async-done(((bf16[1024,3,4,128]{3,0,2,1:T(8,128)(2,1)}), bf16[4096,3,4,128]{3,0,2,1:T(8,128)(2,1)}) %all-gather.7.cloned.1.call-update) | async-done | bytes 12582928 | tf_op jit(solution)/shard_map/all_gather | solution.py:32
  97.5 18.7 %fusion.69 = bf16[3,4,8,55,128]{4,3,1,0,2:T(8,128)(2,1)S(1)} fusion(bf16[4096,3,4,128]{3,0,2,1:T(8,128)(2,1)} %all-gather.7.cloned.1.call-done, f32[4096]{0:T(1024)S(1)} %bitcast.109, f32[4096]{0:T(1024)S(1)} %bitcast.110, f32[8,55]{1,0:T(8,128)S(1)} %add_rsqrt_fusion.1, f32[8,55]{1,0:T(8,128)S(1)} %broadcast_multiply_fusion.1, bf16[8,55,4096]{2,0,1:T(8,128)(2,1)} %param.8), kind=kOutput, calls=%fused_computation.65 | convolution fusion | flops 5547970560 | bytes 17575360 | tf_op jit(solution)/shard_map/fpd,dshe->shfpe/dot_general | solution.py:29
  117.3 3.5 all-to-all-start
  121.7 12.3 %all-to-all-done = bf16[4,8,55,128]{3,1,2,0:T(8,128)(2,1)S(1)} async-done(((bf16[4,8,55,128]{3,1,2,0:T(8,128)(2,1)}), bf16[4,8,55,128]{3,1,2,0:T(8,128)(2,1)S(1)}, u32[]{:S(2)}, u32[]{:S(2)}) %all-to-all-start) | async-done | bytes 450592 | tf_op jit(solution)/shard_map/all_to_all | solution.py:97
  134.0 3.5 all-to-all-start.1
  138.4 7.0 all-to-all-done.1
  145.5 3.5 all-to-all-start.2
  149.1 7.8 all-to-all-done.2
  157.0 4.6 while.10
  162.5 3.5 all-to-all-start.3
  166.1 7.9 all-to-all-done.3
  174.0 4.5 bitcast_convert_fusion
  178.5 3.8 copy.45
  183.7 548.0 %all-gather.15.cloned.1.call-done = bf16[64,55,4096]{2,0,1:T(8,128)(2,1)} async-done(((bf16[8,55,4096]{2,0,1:T(8,128)(2,1)}), bf16[64,55,4096]{2,0,1:T(8,128)(2,1)}) %all-gather.15.cloned.1.call-update) | async-done | bytes 28835856 | tf_op jit(solution)/shard_map/all_gather | solution.py:13
  731.7 14.2 %bitcast_reduce_fusion = bf16[8,55,4096]{2,0,1:T(8,128)(2,1)} fusion(bf16[64,55,4096]{2,0,1:T(8,128)(2,1)} %all-gather.15.cloned.1.call-done), kind=kLoop, calls=%fused_computation.17 | loop fusion | flops 12615680 | bytes 32440320 | tf_op jit(solution)/shard_map/reduce_sum | solution.py:13
  745.9 15.1 %convert_reduce_fusion.1 = (f32[8,55]{1,0:T(8,128)S(1)}, bf16[8,55,4096]{2,1,0:T(8,128)(2,1)S(1)}) fusion(bf16[8,55,4096]{2,0,1:T(8,128)(2,1)} %bitcast_reduce_fusion, f32[4096]{0:T(1024)S(1)} %bitcast.106, bf16[8,55,4096]{2,0,1:T(8,128)(2,1)} %param.8), kind=kLoop, calls=%fused_computation.28 | loop fusion | flops 12615240 | bytes 10831584 | tf_op jit(solution)/shard_map/reduce_sum | solution.py:22
  763.9 75.1 %all-gather.11.cloned.1.call-done = bf16[4096,2048]{1,0:T(8,128)(2,1)} async-done(((bf16[1024,2048]{1,0:T(8,128)(2,1)}), bf16[4096,2048]{1,0:T(8,128)(2,1)}) %all-gather.11.cloned.1.call-update) | async-done | bytes 16777232 | tf_op jit(solution)/shard_map/all_gather | solution.py:32
  839.0 107.3 %all-gather.13.cloned.1.call-done = bf16[2048,4096]{1,0:T(8,128)(2,1)} async-done(((bf16[2048,1024]{1,0:T(8,128)(2,1)}), bf16[2048,4096]{1,0:T(8,128)(2,1)}) %all-gather.13.cloned.1.call-update) | async-done | bytes 16777232 | tf_op jit(solution)/shard_map/all_gather | solution.py:38
  946.3 29.8 %fusion.32 = bf16[8,55,4096]{2,1,0:T(8,128)(2,1)} fusion(bf16[2048,4096]{1,0:T(8,128)(2,1)} %all-gather.13.cloned.1.call-done, bf16[4096,2048]{1,0:T(8,128)(2,1)} %all-gather.11.cloned.1.call-done, bf16[8,55,4096]{2,1,0:T(8,128)(2,1)} %copy-done.1, f32[4096]{0:T(1024)S(1)} %bitcast.107, f32[4096]{0:T(1024)S(1)} %bitcast.108, ...), kind=kOutput, calls=%fused_computation.43 | convolution fusion | flops 14784675840 | bytes 40799680 | tf_op jit(solution)/shard_map/fpk,kc->fpc/dot_general | solution.py:40
  976.2 81.5 %reduce-scatter.2.cloned.1.call-done = bf16[8,55,512]{2,1,0:T(8,128)(2,1)} async-done(((bf16[8,55,4096]{2,1,0:T(8,128)(2,1)}), bf16[8,55,512]{2,1,0:T(8,128)(2,1)}) %reduce-scatter.2.cloned.1.call-update) | async-done | bytes 450576 | tf_op jit(solution)/shard_map/reduce_scatter | solution.py:80
  (61 shorter events, 15.9 us)
Async XLA Ops:
  6.5 91.0 %all-gather.7.cloned.1.call-start = ((), (), s32[]{:S(2)}) async-start(), calls=%async_computation.5 | async-start | bytes 15728640 | tf_op jit(solution)/shard_map/all_gather | solution.py:32
  9.7 3.6 copy-start.2
  12.6 153.5 %all-gather.9.cloned.1.call-start = ((), (), s32[]{:S(2)}) async-start(), calls=%async_computation.6 | async-start | bytes 5242880 | tf_op jit(solution)/shard_map/all_gather | solution.py:38
  13.3 5.9 copy-start
  117.3 16.7 %all-to-all-start = ((bf16[4,8,55,128]{3,1,2,0:T(8,128)(2,1)}), bf16[4,8,55,128]{3,1,2,0:T(8,128)(2,1)S(1)}, u32[]{:S(2)}, u32[]{:S(2)}) async-start(bf16[4,8,55,128]{3,1,2,0:T(8,128)(2,1)} %copy.37), calls=%async_computation | async-start | bytes 901120 | tf_op jit(solution)/shard_map/all_to_all | solution.py:97
  134.0 11.5 %all-to-all-start.1 = ((bf16[4,8,55,128]{3,1,2,0:T(8,128)(2,1)}), bf16[4,8,55,128]{3,1,2,0:T(8,128)(2,1)S(1)}, u32[]{:S(2)}, u32[]{:S(2)}) async-start(bf16[4,8,55,128]{3,1,2,0:T(8,128)(2,1)} %copy.38), calls=%async_computation.1 | async-start | bytes 901120 | tf_op jit(solution)/shard_map/all_to_all | solution.py:98
  145.5 11.5 %all-to-all-start.2 = ((bf16[4,8,55,128]{3,1,2,0:T(8,128)(2,1)}), bf16[4,8,55,128]{3,1,2,0:T(8,128)(2,1)S(1)}, u32[]{:S(2)}, u32[]{:S(2)}) async-start(bf16[4,8,55,128]{3,1,2,0:T(8,128)(2,1)} %copy.39), calls=%async_computation.2 | async-start | bytes 901120 | tf_op jit(solution)/shard_map/all_to_all | solution.py:99
  162.5 11.5 %all-to-all-start.3 = ((bf16[1,8,220,128]{3,1,0,2:T(8,128)(2,1)}), bf16[1,8,220,128]{3,1,0,2:T(8,128)(2,1)S(1)}, u32[]{:S(2)}, u32[]{:S(2)}) async-start(bf16[1,8,220,128]{3,1,0,2:T(8,128)(2,1)} %bitcast.92), calls=%async_computation.3 | async-start | bytes 901120 | tf_op jit(solution)/shard_map/all_to_all | solution.py:102
  166.0 565.7 %all-gather.15.cloned.1.call-start = ((), (), s32[]{:S(2)}) async-start(), calls=%async_computation.10 | async-start | bytes 32440320 | tf_op jit(solution)/shard_map/all_gather | solution.py:13
  182.4 656.7 %all-gather.11.cloned.1.call-start = ((), (), s32[]{:S(2)}) async-start(), calls=%async_computation.7 | async-start | bytes 20971520 | tf_op jit(solution)/shard_map/all_gather | solution.py:32
  182.9 763.4 %all-gather.13.cloned.1.call-start = ((), (), s32[]{:S(2)}) async-start(), calls=%async_computation.8 | async-start | bytes 20971520 | tf_op jit(solution)/shard_map/all_gather | solution.py:38
  183.5 874.2 %reduce-scatter.2.cloned.1.call-start = ((), (), s32[]{:S(2)}) async-start(), calls=%async_computation.9 | async-start | bytes 4128768 | tf_op jit(solution)/shard_map/reduce_scatter | solution.py:80
  761.0 1.8 copy-start.1
Sparse Core Ops, SparseCore 0:
  12.7 84.7 all-gather.6
  99.1 39.2 all-gather.8
  182.5 549.1 all-gather.14
  733.1 105.8 all-gather.10
  840.4 105.8 all-gather.12
  976.3 81.3 reduce-scatter.1
